TPU v7x, 32 devices: a whole 2x2x4 slice. The times are simulated.
32 devices in a mesh: dp: 16 (over z, y, core), tensor: 2 (over x).
Axes of the slice: x: 2, y: 2, z: 4, core: 2. Of those that a mesh axis runs over, the one named last changes fastest.
Arguments:
- tokens: float32 [2, 25600, 512], P(None, ('dp', 'tensor')), may hold values from -6 to 6
- key_mask: int32 [2, 128, 200], P(None, 'dp'), may hold values from 0 to 1, as said below
- expert_ids: int32 [2, 25600, 2], P(None, 'dp'), may hold values from 0 to 31, as said below
- slot_ids: int32 [2, 25600, 2], P(None, 'dp'), may hold values from -1 to 119, as said below
- norm1_gain: float32 [512], P(('dp', 'tensor')), may hold values from 0.25 to 1.75
- norm1_bias: float32 [512], P(('dp', 'tensor')), may hold values from -3 to 3
- qkv_weight: bfloat16 [512, 3, 512], P('dp', None, 'tensor'), may hold values from -0.25 to 0.25
- out_weight: bfloat16 [512, 512], P('tensor', 'dp'), may hold values from -1 to 1
- norm2_gain: float32 [512], P(('dp', 'tensor')), may hold values from 0.25 to 1.75
- norm2_bias: float32 [512], P(('dp', 'tensor')), may hold values from -3 to 3
- router_weight: float32 [512, 32], P(('dp', 'tensor')), may hold values from -0.25 to 0.25
- expert_in: bfloat16 [32, 512, 2048], P(None, 'dp', 'tensor'), may hold values from -0.25 to 0.25
- expert_out: bfloat16 [32, 2048, 512], P(None, 'tensor', 'dp'), may hold values from -3 to 3
- cotangent: float32 [2, 25600, 512], P(None, ('dp', 'tensor')), may hold values from -6 to 6
Outputs:
- block_out: float32 [2, 25600, 512], P(None, ('dp', 'tensor'))
- input_grad: float32 [2, 25600, 512], P(None, ('dp', 'tensor'))
- norm1_gain_grad: float32 [512], P(('dp', 'tensor'))
- norm1_bias_grad: float32 [512], P(('dp', 'tensor'))
- qkv_grad: float32 [512, 3, 512], P('dp', None, 'tensor')
- out_grad: float32 [512, 512], P('tensor', 'dp')
- norm2_gain_grad: float32 [512], P(('dp', 'tensor'))
- norm2_bias_grad: float32 [512], P(('dp', 'tensor'))
- router_grad: float32 [512, 32], P(('dp', 'tensor'))
- expert_in_grad: float32 [32, 512, 2048], P(None, 'dp', 'tensor')
- expert_out_grad: float32 [32, 2048, 512], P(None, 'tensor', 'dp')
Inputs may be any that keep to these rules, and one draw needn't show every extreme that they name: `key_mask`: position 0 of every image is 1; positions 197 to 199 are 0. `expert_ids`: each row names two different experts. `slot_ids`: slots count within routing groups of 1600 consecutive rows of a micro-batch. -1 marks a dropped route; no two other routes of a group share expert and slot, and the slots used by one expert in a group are 0, 1, 2, ... without gaps.
All inputs are finite; a program needn't handle non-finite values.
Results may differ from a plain program's by a relative error of at most 0.035.
Values may be sent and summed in bfloat16 or wider, within the bound.
A program may use at most 264 MiB of HBM per device.

v0:
```python
import jax
import jax.numpy as jnp
from jax import lax
from jax.sharding import PartitionSpec as P

HEAD = 64
CAP = 120
EPSILON = 1e-06
FIRST_DIMS = (((0,), (0,)), ((), ()))
LAST_DIMS = (((1,), (1,)), ((), ()))


def norm_rows(values, gain, offset):
    center = jnp.mean(values, -1, keepdims=True)
    shifted = values - center
    spread = jnp.mean(shifted * shifted, -1, keepdims=True)
    return shifted * lax.rsqrt(spread + EPSILON) * gain + offset


def slot_table(routes, slot_count):
    places = lax.broadcasted_iota(jnp.int32, (routes.shape[0], slot_count), 1)
    hits = (routes[:, 0:1] == places) | (routes[:, 1:2] == places)
    return hits.astype(jnp.bfloat16)


def per_device(
    tokens,
    key_mask,
    expert_ids,
    slot_ids,
    norm1_gain,
    norm1_bias,
    qkv_weight,
    out_weight,
    norm2_gain,
    norm2_bias,
    router_weight,
    expert_in,
    expert_out,
    cotangent,
):
    highest = lax.Precision.HIGHEST
    gain_one, bias_one, gain_two, bias_two, router_full = (
        lax.all_gather(norm1_gain, ("dp", "tensor"), axis=0, tiled=True),
        lax.all_gather(norm1_bias, ("dp", "tensor"), axis=0, tiled=True),
        lax.all_gather(norm2_gain, ("dp", "tensor"), axis=0, tiled=True),
        lax.all_gather(norm2_bias, ("dp", "tensor"), axis=0, tiled=True),
        lax.all_gather(router_weight, ("dp", "tensor"), axis=0, tiled=True),
    )
    micro_count, own_rows, model_width = tokens.shape
    image_count, seq_length = (key_mask.shape[1], key_mask.shape[2])
    group_rows = image_count * seq_length
    expert_count = expert_in.shape[0]
    hidden_width = expert_in.shape[2]
    slot_count = expert_count * CAP
    head_width = qkv_weight.shape[2]
    local_heads = head_width // HEAD
    scaling = HEAD ** (-0.5)
    own_start = lax.axis_index("tensor") * own_rows

    def fetch_attention():
        qkv_full, attn_full = (
            lax.all_gather(qkv_weight, "dp", axis=0, tiled=True),
            lax.all_gather(out_weight, "dp", axis=1, tiled=True),
        )
        qkv_every, attn_every = (None, None)
        return (qkv_full.reshape(model_width, 3 * head_width), attn_full, qkv_every, attn_every)

    def current_weights():
        return (
            fetch_attention(),
            (
                lax.all_gather(expert_in, "dp", axis=1, tiled=True),
                lax.all_gather(expert_out, "dp", axis=2, tiled=True),
            ),
        )

    qkv_acc = jnp.zeros((model_width, 3 * head_width), jnp.float32)
    attn_acc = jnp.zeros((head_width, model_width), jnp.float32)
    first_acc = jnp.zeros((expert_count, model_width, hidden_width), jnp.float32)
    second_acc = jnp.zeros((expert_count, hidden_width, model_width), jnp.float32)
    router_acc = jnp.zeros((model_width, expert_count), jnp.float32)
    gain_one_acc = jnp.zeros((model_width,), jnp.float32)
    bias_one_acc = jnp.zeros((model_width,), jnp.float32)
    gain_two_acc = jnp.zeros((model_width,), jnp.float32)
    bias_two_acc = jnp.zeros((model_width,), jnp.float32)
    block_list = []
    grad_list = []
    for micro_step in range(micro_count):
        row_block = tokens[micro_step]
        cot_block = cotangent[micro_step]
        key_flags = key_mask[micro_step]
        experts = expert_ids[micro_step]
        places = slot_ids[micro_step]
        retained = (places >= 0).astype(jnp.float32)
        slot_index = jnp.where(places >= 0, experts * CAP + places, slot_count)

        def masked_scores(query, keyed):
            raw = (
                jnp.einsum("bqhd,bkhd->bhqk", query, keyed, preferred_element_type=jnp.float32)
                * scaling
            )
            return jnp.where(key_flags[:, None, None, :] > 0, raw, -1e30)

        (qkv_joined, attn_local, qkv_every, attn_every), (first_layer, second_layer) = (
            current_weights()
        )
        normed_own = norm_rows(row_block, gain_one, bias_one).astype(jnp.bfloat16)
        normed_all = lax.all_gather(normed_own, "tensor", axis=0, tiled=True)
        projected = jnp.dot(normed_all, qkv_joined, preferred_element_type=jnp.float32).astype(
            jnp.bfloat16
        )
        projected = projected.reshape(image_count, seq_length, 3, local_heads, HEAD)
        query, keyed, valued = (projected[:, :, 0], projected[:, :, 1], projected[:, :, 2])
        scores = masked_scores(query, keyed)
        row_max = jnp.max(scores, -1, keepdims=True)
        lifted = jnp.exp(scores - row_max)
        row_total = jnp.sum(lifted, -1, keepdims=True)
        probs = lifted / row_total
        log_total = row_max + jnp.log(row_total)
        mixed = jnp.einsum(
            "bhqk,bkhd->bqhd",
            probs.astype(jnp.bfloat16),
            valued,
            preferred_element_type=jnp.float32,
        )
        mixed = mixed.astype(jnp.bfloat16).reshape(group_rows, head_width)
        middle = row_block + lax.psum_scatter(
            jnp.dot(mixed, attn_local, preferred_element_type=jnp.float32).astype(jnp.bfloat16),
            "tensor",
            scatter_dimension=0,
            tiled=True,
        ).astype(jnp.float32)
        routed_own = norm_rows(middle, gain_two, bias_two).astype(jnp.bfloat16)
        piece = lax.all_gather(routed_own, "tensor", axis=0, tiled=True)
        count = piece.shape[0]
        gates = jax.nn.softmax(
            jnp.dot(piece.astype(jnp.float32), router_full, precision=highest), axis=-1
        )
        picks = lax.broadcasted_iota(jnp.int32, (count, 2, expert_count), 2) == experts[:, :, None]
        picked_gates = jnp.sum(jnp.where(picks, gates[:, None, :], 0.0), -1) * retained
        chosen = picked_gates
        table = slot_table(slot_index, slot_count)
        dispatched = lax.dot_general(table, piece, FIRST_DIMS, preferred_element_type=jnp.float32)
        dispatched, chosen = (dispatched, chosen)
        slot_gate = (
            jnp.zeros((slot_count + 1,), jnp.float32)
            .at[slot_index.reshape(-1)]
            .set(chosen.reshape(-1))[:slot_count]
        )
        dispatched_low = dispatched.astype(jnp.bfloat16).reshape(expert_count, CAP, model_width)
        hidden_pre = jnp.einsum(
            "ecd,edf->ecf", dispatched_low, first_layer, preferred_element_type=jnp.float32
        )
        hidden = jax.nn.gelu(hidden_pre).astype(jnp.bfloat16)
        expert_part = jnp.einsum(
            "ecf,efd->ecd", hidden, second_layer, preferred_element_type=jnp.float32
        ).reshape(slot_count, model_width)
        weighted = jnp.concatenate(
            [slot_gate[:, None] * expert_part, jnp.zeros((1, model_width), jnp.float32)], 0
        )
        block_list.append(
            middle
            + lax.psum_scatter(
                (weighted[slot_index[:, 0]] + weighted[slot_index[:, 1]]).astype(jnp.bfloat16),
                "tensor",
                scatter_dimension=0,
                tiled=True,
            ).astype(jnp.float32)
        )
        (qkv_joined, attn_local, qkv_every, attn_every), (first_layer, second_layer) = (
            current_weights()
        )
        cot_low = cot_block.astype(jnp.bfloat16)
        picked_grads = lax.dot_general(
            slot_table(slot_index, slot_count),
            lax.all_gather(cot_low, "tensor", axis=0, tiled=True),
            FIRST_DIMS,
            preferred_element_type=jnp.float32,
        )
        gate_part = jnp.sum(picked_grads * expert_part, -1)
        result_grad = (
            (slot_gate[:, None] * picked_grads)
            .astype(jnp.bfloat16)
            .reshape(expert_count, CAP, model_width)
        )
        hidden_grad = jnp.einsum(
            "ecd,efd->ecf", result_grad, second_layer, preferred_element_type=jnp.float32
        )
        pre_grad = jax.vjp(jax.nn.gelu, hidden_pre)[1](hidden_grad)[0].astype(jnp.bfloat16)
        first_acc = first_acc + jnp.einsum(
            "ecd,ecf->edf", dispatched_low, pre_grad, preferred_element_type=jnp.float32
        )
        second_acc = second_acc + jnp.einsum(
            "ecf,ecd->efd", hidden, result_grad, preferred_element_type=jnp.float32
        )
        dispatch_grad = jnp.einsum(
            "ecf,edf->ecd", pre_grad, first_layer, preferred_element_type=jnp.float32
        ).reshape(slot_count, model_width)
        dispatch_grad = jnp.concatenate(
            [dispatch_grad, jnp.zeros((1, model_width), jnp.float32)], 0
        )
        gate_padded = jnp.concatenate([gate_part, jnp.zeros((1,), jnp.float32)], 0)
        row_grads = dispatch_grad[slot_index[:, 0]] + dispatch_grad[slot_index[:, 1]]
        gate_grads = gate_padded[slot_index]
        own_row_grads, own_gate_grads = (
            lax.psum_scatter(
                row_grads.astype(jnp.bfloat16), "tensor", scatter_dimension=0, tiled=True
            ).astype(jnp.float32),
            lax.psum_scatter(
                gate_grads.astype(jnp.bfloat16), "tensor", scatter_dimension=0, tiled=True
            ).astype(jnp.float32),
        )
        own_experts = lax.dynamic_slice_in_dim(experts, own_start, own_rows, 0)
        routed_wide = routed_own.astype(jnp.float32)
        own_gates = jax.nn.softmax(jnp.dot(routed_wide, router_full, precision=highest), axis=-1)
        own_picks = (
            lax.broadcasted_iota(jnp.int32, (own_rows, 2, expert_count), 2)
            == own_experts[:, :, None]
        )
        gate_cot = jnp.sum(jnp.where(own_picks, own_gate_grads[:, :, None], 0.0), 1)
        logit_grad = own_gates * (gate_cot - jnp.sum(own_gates * gate_cot, -1, keepdims=True))
        routed_grad = own_row_grads + jnp.dot(logit_grad, router_full.T, precision=highest)
        router_acc = router_acc + jnp.dot(routed_wide.T, logit_grad, precision=highest)
        middle_part, gain_step, bias_step = jax.vjp(norm_rows, middle, gain_two, bias_two)[1](
            routed_grad
        )
        gain_two_acc = gain_two_acc + gain_step
        bias_two_acc = bias_two_acc + bias_step
        middle_grad = cot_block + middle_part
        attn_cot = lax.all_gather(middle_grad.astype(jnp.bfloat16), "tensor", axis=0, tiled=True)
        attn_acc = attn_acc + lax.dot_general(
            mixed, attn_cot, FIRST_DIMS, preferred_element_type=jnp.float32
        )
        mixed_grad = lax.dot_general(
            attn_cot, attn_local, LAST_DIMS, preferred_element_type=jnp.float32
        )
        mixed_grad = mixed_grad.astype(jnp.bfloat16).reshape(
            image_count, seq_length, local_heads, HEAD
        )
        again_probs = jnp.exp(masked_scores(query, keyed) - log_total)
        prob_grad = jnp.einsum(
            "bqhd,bkhd->bhqk", mixed_grad, valued, preferred_element_type=jnp.float32
        )
        value_grad = jnp.einsum(
            "bhqk,bqhd->bkhd",
            again_probs.astype(jnp.bfloat16),
            mixed_grad,
            preferred_element_type=jnp.float32,
        ).astype(jnp.bfloat16)
        inner_sum = jnp.sum(again_probs * prob_grad, -1, keepdims=True)
        score_grad = (again_probs * (prob_grad - inner_sum)).astype(jnp.bfloat16)
        query_grad = (
            jnp.einsum("bhqk,bkhd->bqhd", score_grad, keyed, preferred_element_type=jnp.float32)
            * scaling
        ).astype(jnp.bfloat16)
        keyed_grad = (
            jnp.einsum("bhqk,bqhd->bkhd", score_grad, query, preferred_element_type=jnp.float32)
            * scaling
        ).astype(jnp.bfloat16)
        proj_grad = jnp.stack([query_grad, keyed_grad, value_grad], 2).reshape(
            group_rows, 3 * head_width
        )
        qkv_acc = qkv_acc + lax.dot_general(
            normed_all, proj_grad, FIRST_DIMS, preferred_element_type=jnp.float32
        )
        normed_grad = lax.psum_scatter(
            lax.dot_general(
                proj_grad, qkv_joined, LAST_DIMS, preferred_element_type=jnp.float32
            ).astype(jnp.bfloat16),
            "tensor",
            scatter_dimension=0,
            tiled=True,
        ).astype(jnp.float32)
        input_part, gain_step, bias_step = jax.vjp(norm_rows, row_block, gain_one, bias_one)[1](
            normed_grad
        )
        gain_one_acc = gain_one_acc + gain_step
        bias_one_acc = bias_one_acc + bias_step
        grad_list.append(middle_grad + input_part)
    qkv_grad, out_grad, first_grad, second_grad = (
        lax.psum_scatter(
            qkv_acc.reshape(model_width, 3, head_width).astype(jnp.bfloat16),
            "dp",
            scatter_dimension=0,
            tiled=True,
        ).astype(jnp.float32),
        lax.psum_scatter(
            attn_acc.astype(jnp.bfloat16), "dp", scatter_dimension=1, tiled=True
        ).astype(jnp.float32),
        lax.psum_scatter(
            first_acc.astype(jnp.bfloat16), "dp", scatter_dimension=1, tiled=True
        ).astype(jnp.float32),
        lax.psum_scatter(
            second_acc.astype(jnp.bfloat16), "dp", scatter_dimension=2, tiled=True
        ).astype(jnp.float32),
    )
    gain_one_grad, bias_one_grad, gain_two_grad, bias_two_grad, router_grad = (
        lax.psum_scatter(gain_one_acc, ("dp", "tensor"), scatter_dimension=0, tiled=True),
        lax.psum_scatter(bias_one_acc, ("dp", "tensor"), scatter_dimension=0, tiled=True),
        lax.psum_scatter(gain_two_acc, ("dp", "tensor"), scatter_dimension=0, tiled=True),
        lax.psum_scatter(bias_two_acc, ("dp", "tensor"), scatter_dimension=0, tiled=True),
        lax.psum_scatter(router_acc, ("dp", "tensor"), scatter_dimension=0, tiled=True),
    )
    return (
        jnp.stack(block_list),
        jnp.stack(grad_list),
        gain_one_grad,
        bias_one_grad,
        qkv_grad,
        out_grad,
        gain_two_grad,
        bias_two_grad,
        router_grad,
        first_grad,
        second_grad,
    )


def solution(mesh):
    placed = (
        P(None, ("dp", "tensor"), None),
        P(None, "dp", None),
        P(None, "dp", None),
        P(None, "dp", None),
        P(("dp", "tensor")),
        P(("dp", "tensor")),
        P("dp", None, "tensor"),
        P("tensor", "dp"),
        P(("dp", "tensor")),
        P(("dp", "tensor")),
        P(("dp", "tensor"), None),
        P(None, "dp", "tensor"),
        P(None, "tensor", "dp"),
        P(None, ("dp", "tensor"), None),
    )
    return jax.shard_map(
        per_device,
        mesh=mesh,
        in_specs=placed,
        out_specs=(
            P(None, ("dp", "tensor"), None),
            P(None, ("dp", "tensor"), None),
            P(("dp", "tensor")),
            P(("dp", "tensor")),
            P("dp", None, "tensor"),
            P("tensor", "dp"),
            P(("dp", "tensor")),
            P(("dp", "tensor")),
            P(("dp", "tensor"), None),
            P(None, "dp", "tensor"),
            P(None, "tensor", "dp"),
        ),
        check_vma=False,
    )
```

profile of v0, /device:TPU:0, one launch (start us, length us, event | category | flops | bytes accessed | tf_op | source)
XLA Modules:
  0.0 2154.3 jit_solution(1419710168144649038)
XLA Ops:
  12.3 42.0 %all-reduce.14 = (f32[512]{0:T(512)S(1)}, f32[512]{0:T(512)S(1)}, f32[512]{0:T(512)S(1)}, f32[512]{0:T(512)S(1)}) all-reduce(f32[512]{0:T(512)S(1)} %dynamic-update-slice.1, f32[512]{0:T(512)S(1)} %dynamic-update-slice, f32[512]{0:T(512)S(1)} %dynamic-update-slice.3, ...), channel_id=1, replica_groups=mesh['dp'=16,'tensor'=2] {'dp','tensor'}, use_global_device_ids=true, to_apply=%add.5 | all-reduce | flops 2048 | bytes 16384
  56.8 22.0 %all_gather.67 = bf16[256,512]{0,1:T(8,128)(2,1)S(1)} all-gather(bf16[256,32]{0,1:T(8,128)(2,1)} %param.21), channel_id=1, replica_groups=mesh['dp'=16,'tensor'=2] {'dp'}, dimensions={1}, use_global_device_ids=true | all-gather | bytes 278528 | tf_op jit(solution)/shard_map/all_gather | solution.py:64
  78.8 21.7 %all_gather.66 = bf16[512,3,256]{2,0,1:T(8,128)(2,1)} all-gather(bf16[32,3,256]{2,0,1:T(8,128)(2,1)} %param.20), channel_id=1, replica_groups=mesh['dp'=16,'tensor'=2] {'dp'}, dimensions={0}, use_global_device_ids=true | all-gather | bytes 835584 | tf_op jit(solution)/shard_map/all_gather | solution.py:63
  107.4 8.2 reshape.604
  151.3 8.2 reshape.605
  190.5 24.6 %reduce-scatter.23.cloned.1.call-done = bf16[800,512]{1,0:T(8,128)(2,1)} async-done(((bf16[1600,512]{1,0:T(8,128)(2,1)}), bf16[800,512]{1,0:T(8,128)(2,1)}) %reduce-scatter.23.cloned.1.call-update) | async-done | bytes 819216 | tf_op jit(solution)/shard_map/reduce_scatter | solution.py:128
  228.6 69.3 %all_gather.71 = f32[512,32]{1,0:T(8,128)S(1)} all-gather(f32[16,32]{1,0:T(8,128)S(1)} %copy-done.106), channel_id=1, replica_groups=mesh['dp'=16,'tensor'=2] {'dp','tensor'}, dimensions={0}, use_global_device_ids=true | all-gather | bytes 67584 | tf_op jit(solution)/shard_map/all_gather | solution.py:48
  310.7 16.4 scatter_custom_fusion
  327.1 16.2 scatter_custom_fusion.1
  343.4 10.5 fusion.34
  353.8 10.7 fusion.37
  364.6 87.7 %all-gather.15.cloned.1.call-done = bf16[32,512,1024]{2,1,0:T(8,128)(2,1)} async-done(((bf16[32,32,1024]{2,1,0:T(8,128)(2,1)}), bf16[32,512,1024]{2,1,0:T(8,128)(2,1)}) %all-gather.15.cloned.1.call-update) | async-done | bytes 33554448 | tf_op jit(solution)/shard_map/all_gather | solution.py:73
  452.2 21.3 fusion.145
  473.5 148.3 %all-gather.17.cloned.1.call-done = bf16[32,1024,512]{1,2,0:T(8,128)(2,1)} async-done(((bf16[32,1024,32]{1,2,0:T(8,128)(2,1)}), bf16[32,1024,512]{1,2,0:T(8,128)(2,1)}) %all-gather.17.cloned.1.call-update) | async-done | bytes 33554448 | tf_op jit(solution)/shard_map/all_gather | solution.py:74
  621.8 23.1 %fusion.130 = f32[32,120,512]{2,1,0:T(8,128)} fusion(bf16[32,1024,512]{1,2,0:T(8,128)(2,1)} %all-gather.17.cloned.1.call-done, f32[32,120,1024]{2,1,0:T(8,128)} %fusion.145), kind=kOutput, calls=%fused_computation.282 | convolution fusion | flops 4061921280 | bytes 57147392 | tf_op jit(solution)/shard_map/ecf,efd->ecd/dot_general | solution.py:156
  651.9 17.7 fusion.32
  669.6 19.2 gather_fusion.9
  690.5 20.8 fusion.144
  711.3 22.2 %fusion.129 = f32[32,120,512]{2,1,0:T(8,128)} fusion(bf16[32,1024,512]{1,2,0:T(8,128)(2,1)} %all-gather.17.cloned.1.call-done, f32[32,120,1024]{2,1,0:T(8,128)} %fusion.144), kind=kOutput, calls=%fused_computation.281 | convolution fusion | flops 4061921280 | bytes 57147392 | tf_op jit(solution)/shard_map/ecf,efd->ecd/dot_general | solution.py:156
  733.6 16.6 fusion.33
  752.0 24.5 %fusion.16 = bf16[32,120,1024]{2,1,0:T(8,128)(2,1)} fusion(f32[32,120,1024]{2,1,0:T(8,128)} %fusion.144, bf16[32,120,512]{2,1,0:T(8,128)(2,1)S(1)} %bitcast.286, bf16[32,1024,512]{1,2,0:T(8,128)(2,1)} %all-gather.17.cloned.1.call-done), kind=kOutput, calls=%fused_computation.34 | convolution fusion | flops 4105175040 | bytes 61079552 | tf_op jit(solution)/shard_map/ecd,efd->ecf/dot_general | solution.py:187
  776.6 21.0 fusion.146
  797.6 19.2 gather_fusion.6
  818.4 7.3 concatenate.20
  825.7 9.0 gather_fusion.5
  834.8 9.6 gather_fusion.4
  848.1 24.2 %fusion.23 = bf16[32,120,1024]{2,1,0:T(8,128)(2,1)} fusion(f32[32,120,1024]{2,1,0:T(8,128)} %fusion.145, bf16[32,120,512]{2,1,0:T(8,128)(2,1)} %bitcast.288, bf16[32,1024,512]{1,2,0:T(8,128)(2,1)} %all-gather.17.cloned.1.call-done), kind=kOutput, calls=%fused_computation.41 | convolution fusion | flops 4105175040 | bytes 61079552 | tf_op jit(solution)/shard_map/ecd,efd->ecf/dot_general | solution.py:187
  872.3 21.0 fusion.147
  893.4 7.3 concatenate.22
  900.7 9.0 gather_fusion.8
  909.7 9.6 gather_fusion.7
  930.4 9.4 gather_fusion.3
  939.8 9.6 gather_fusion.2
  960.5 9.0 gather_fusion.1
  969.6 9.6 gather_fusion
  1020.4 27.1 %all-gather.25.cloned.1.call-done = bf16[1600,512]{1,0:T(8,128)(2,1)} async-done(((bf16[800,512]{1,0:T(8,128)(2,1)}), bf16[1600,512]{1,0:T(8,128)(2,1)}) %all-gather.25.cloned.1.call-update) | async-done | bytes 1638416 | tf_op jit(solution)/shard_map/all_gather | solution.py:231
  1051.2 7.5 multiply_reduce_fusion.1
  1069.3 8.0 all-gather.29.cloned.1.call-done
  1139.9 30.2 %fusion.128 = f32[32,1024,512]{1,2,0:T(8,128)} fusion(bf16[32,120,512]{2,1,0:T(8,128)(2,1)} %bitcast.287, f32[32,120,1024]{2,1,0:T(8,128)} %fusion.144), kind=kOutput, calls=%fused_computation.280 | convolution fusion | flops 4061921280 | bytes 86769664 | tf_op jit(solution)/shard_map/ecf,ecd->efd/dot_general | solution.py:194
  1172.9 40.5 %add_convert_fusion = bf16[32,1024,512]{1,2,0:T(8,128)(2,1)} fusion(f32[32,1024,512]{1,2,0:T(8,128)} %fusion.128, bf16[32,120,512]{2,1,0:T(8,128)(2,1)} %bitcast.289, f32[32,120,1024]{2,1,0:T(8,128)} %fusion.145), kind=kOutput, calls=%fused_computation.12 | convolution fusion | flops 4095475712 | bytes 120324096 | tf_op jit(solution)/shard_map/ecf,ecd->efd/dot_general | solution.py:194
  1213.4 27.6 %fusion.150 = f32[32,512,1024]{2,1,0:T(8,128)} fusion(bf16[32,120,512]{2,1,0:T(8,128)(2,1)} %bitcast.285, bf16[32,120,1024]{2,1,0:T(8,128)(2,1)} %fusion.16), kind=kOutput, calls=%fused_computation.302 | convolution fusion | flops 4026531840 | bytes 78905344 | tf_op jit(solution)/shard_map/ecd,ecf->edf/dot_general | solution.py:191
  1241.1 37.5 %add_convert_fusion.1 = bf16[32,512,1024]{2,1,0:T(8,128)(2,1)} fusion(f32[32,512,1024]{2,1,0:T(8,128)} %fusion.150, bf16[32,120,512]{2,1,0:T(8,128)(2,1)} %bitcast.283, bf16[32,120,1024]{2,1,0:T(8,128)(2,1)} %fusion.23), kind=kOutput, calls=%fused_computation.13 | convolution fusion | flops 4060086272 | bytes 112459776 | tf_op jit(solution)/shard_map/ecd,ecf->edf/dot_general | solution.py:191
  1290.6 21.1 reduce-scatter.29.cloned.1.call-done
  1311.7 29.7 %reduce-scatter.33.cloned.1.call-done = bf16[800,512]{1,0:T(8,128)(2,1)} async-done(((bf16[1600,512]{1,0:T(8,128)(2,1)}), bf16[800,512]{1,0:T(8,128)(2,1)}) %reduce-scatter.33.cloned.1.call-update) | async-done | bytes 819216 | tf_op jit(solution)/shard_map/reduce_scatter | solution.py:267
  1345.8 39.4 %all-reduce.13 = (f32[512]{0:T(512)S(1)}, f32[512]{0:T(512)S(1)}, f32[512]{0:T(512)S(1)}, f32[512]{0:T(512)S(1)}) all-reduce(f32[512]{0:T(512)S(1)} %add.372, f32[512]{0:T(512)S(1)} %add.373, f32[512]{0:T(512)S(1)} %add.376, f32[512]{0:T(512)S(1)} %add.377), channel_id=12, replica_groups=mesh['dp'=16,'tensor'=2] {'dp','tensor'}, use_global_device_ids=true, to_apply=%region_52.53.clone | all-reduce | flops 2048 | bytes 16384
  1395.1 281.1 %reduce-scatter.41.cloned.1.call-done = bf16[32,1024,32]{1,2,0:T(8,128)(2,1)} async-done(((bf16[32,1024,512]{1,2,0:T(8,128)(2,1)}), bf16[32,1024,32]{1,2,0:T(8,128)(2,1)}) %reduce-scatter.41.cloned.1.call-update) | async-done | bytes 2097168 | tf_op jit(solution)/shard_map/reduce_scatter | solution.py:294
  1680.4 329.7 %reduce-scatter.39.cloned.1.call-done = bf16[32,32,1024]{2,1,0:T(8,128)(2,1)} async-done(((bf16[32,512,1024]{2,1,0:T(8,128)(2,1)}), bf16[32,32,1024]{2,1,0:T(8,128)(2,1)}) %reduce-scatter.39.cloned.1.call-update) | async-done | bytes 2097168 | tf_op jit(solution)/shard_map/reduce_scatter | solution.py:291
  2014.1 133.5 %reduce-scatter.37.cloned.1.call-done = f32[16,32]{1,0:T(8,128)} async-done(((f32[512,32]{1,0:T(8,128)}), f32[16,32]{1,0:T(8,128)}) %reduce-scatter.37.cloned.1.call-update) | async-done | bytes 2064 | tf_op jit(solution)/shard_map/reduce_scatter | solution.py:303
  (481 shorter events, 298.5 us)
Async XLA Ops:
  7.2 95.6 %all-gather.11.cloned.1.call-start = ((), (), s32[]{:S(2)}) async-start(), calls=%async_computation.14 | async-start | bytes 2457600 | tf_op jit(solution)/shard_map/all_gather | solution.py:109
  9.7 46.2 %copy-start.53 = (f32[800]{0:T(1024)}, f32[800]{0:T(1024)S(1)}, u32[]{:S(2)}) copy-start(f32[800]{0:T(1024)S(1)} %get-tuple-element.176) | copy-start | bytes 9604
  9.7 46.2 %copy-start.55 = (f32[800]{0:T(1024)}, f32[800]{0:T(1024)S(1)}, u32[]{:S(2)}) copy-start(f32[800]{0:T(1024)S(1)} %get-tuple-element.177) | copy-start | bytes 9604
  11.3 45.4 %copy-start.76 = (f32[800]{0:T(1024)}, f32[800]{0:T(1024)S(1)}, u32[]{:S(2)}) copy-start(f32[800]{0:T(1024)S(1)} %fusion.118) | copy-start | bytes 9604
  11.3 45.4 %copy-start.78 = (f32[800]{0:T(1024)}, f32[800]{0:T(1024)S(1)}, u32[]{:S(2)}) copy-start(f32[800]{0:T(1024)S(1)} %fusion.120) | copy-start | bytes 9604
  54.3 165.0 %copy-start.99 = (f32[512]{0:T(512)}, f32[512]{0:T(512)S(1)}, u32[]{:S(2)}) copy-start(f32[512]{0:T(512)S(1)} %get-tuple-element.101) | copy-start | bytes 6148
  56.0 90.8 %all-gather.19.cloned.1.call-start = ((), (), s32[]{:S(2)}) async-start(), calls=%async_computation.20 | async-start | bytes 2457600 | tf_op jit(solution)/shard_map/all_gather | solution.py:109
  56.7 133.8 %reduce-scatter.19.cloned.1.call-start = ((), (), s32[]{:S(2)}) async-start(), calls=%async_computation.15 | async-start | bytes 2457600 | tf_op jit(solution)/shard_map/reduce_scatter | solution.py:128
  78.8 108.7 %copy-start.27 = (bf16[256,512]{0,1:T(8,128)(2,1)}, bf16[256,512]{0,1:T(8,128)(2,1)S(1)}, u32[]{:S(2)}) copy-start(bf16[256,512]{0,1:T(8,128)(2,1)S(1)} %all_gather.67) | copy-start | bytes 786436
  146.5 68.6 %reduce-scatter.23.cloned.1.call-start = ((), (), s32[]{:S(2)}) async-start(), calls=%async_computation.21 | async-start | bytes 2457600 | tf_op jit(solution)/shard_map/reduce_scatter | solution.py:128
  190.5 112.4 %all-gather.21.cloned.1.call-start = ((), (), s32[]{:S(2)}) async-start(), calls=%async_computation.22 | async-start | bytes 2457600 | tf_op jit(solution)/shard_map/all_gather | solution.py:135
  221.6 84.3 %all-gather.13.cloned.1.call-start = ((), (), s32[]{:S(2)}) async-start(), calls=%async_computation.16 | async-start | bytes 2457600 | tf_op jit(solution)/shard_map/all_gather | solution.py:135
  222.1 230.1 %all-gather.15.cloned.1.call-start = ((), (), s32[]{:S(2)}) async-start(), calls=%async_computation.17 | async-start | bytes 35651584 | tf_op jit(solution)/shard_map/all_gather | solution.py:73
  222.9 398.9 %all-gather.17.cloned.1.call-start = ((), (), s32[]{:S(2)}) async-start(), calls=%async_computation.18 | async-start | bytes 35651584 | tf_op jit(solution)/shard_map/all_gather | solution.py:74
  223.7 428.2 %all-gather.27.cloned.1.call-start = ((), (), s32[]{:S(2)}) async-start(), calls=%async_computation.28 | async-start | bytes 2457600 | tf_op jit(solution)/shard_map/all_gather | solution.py:177
  225.1 508.4 %all-gather.23.cloned.1.call-start = ((), (), s32[]{:S(2)}) async-start(), calls=%async_computation.24 | async-start | bytes 2457600 | tf_op jit(solution)/shard_map/all_gather | solution.py:177
  225.7 766.2 %reduce-scatter.45.cloned.1.call-start = ((), (), s32[]{:S(2)}) async-start(), calls=%async_computation.37 | async-start | bytes 614400
  226.6 116.7 %copy-start.107 = (s32[1600]{0:T(1024)}, s32[1600]{0:T(1024)S(1)}, u32[]{:S(2)}) copy-start(s32[1600]{0:T(1024)S(1)} %get-tuple-element.88) | copy-start | bytes 19204
  226.6 116.7 %copy-start.109 = (s32[1600]{0:T(1024)}, s32[1600]{0:T(1024)S(1)}, u32[]{:S(2)}) copy-start(s32[1600]{0:T(1024)S(1)} %get-tuple-element.89) | copy-start | bytes 19204
  305.9 37.5 %copy-start.46 = (bf16[1600,512]{1,0:T(8,128)(2,1)S(1)}, bf16[1600,512]{1,0:T(8,128)(2,1)}, u32[]{:S(2)}) copy-start(bf16[1600,512]{1,0:T(8,128)(2,1)} %all-gather.13.cloned.1.call-done) | copy-start | bytes 4915204
  690.5 304.4 %reduce-scatter.43.cloned.1.call-start = ((), (), s32[]{:S(2)}) async-start(), calls=%async_computation.36 | async-start | bytes 614400
  711.3 22.3 %copy-start.110 = (s32[1600]{0:T(1024)S(1)}, s32[1600]{0:T(1024)}, u32[]{:S(2)}) copy-start(s32[1600]{0:T(1024)} %copy-done.109) | copy-start | bytes 19204
  844.3 157.5 %reduce-scatter.27.cloned.1.call-start = ((), (), s32[]{:S(2)}) async-start(), calls=%async_computation.25 | async-start | bytes 2457600 | tf_op jit(solution)/shard_map/reduce_scatter | solution.py:207
  848.1 157.8 %reduce-scatter.31.cloned.1.call-start = ((), (), s32[]{:S(2)}) async-start(), calls=%async_computation.29 | async-start | bytes 2457600 | tf_op jit(solution)/shard_map/reduce_scatter | solution.py:207
  923.0 88.9 %reduce-scatter.25.cloned.1.call-start = ((), (), s32[]{:S(2)}) async-start(), calls=%async_computation.23 | async-start | bytes 2457600 | tf_op jit(solution)/shard_map/reduce_scatter | solution.py:164
  953.2 58.8 %reduce-scatter.21.cloned.1.call-start = ((), (), s32[]{:S(2)}) async-start(), calls=%async_computation.19 | async-start | bytes 2457600 | tf_op jit(solution)/shard_map/reduce_scatter | solution.py:164
  983.0 64.4 %all-gather.25.cloned.1.call-start = ((), (), s32[]{:S(2)}) async-start(), calls=%async_computation.26 | async-start | bytes 2457600 | tf_op jit(solution)/shard_map/all_gather | solution.py:231
  987.3 24.6 %copy-start.64 = (f32[800]{0:T(1024)}, f32[800]{0:T(1024)S(1)}, u32[]{:S(2)}) copy-start(f32[800]{0:T(1024)S(1)} %get-tuple-element.169) | copy-start | bytes 9604
  1017.4 30.0 %copy-start.28 = (bf16[256,512]{0,1:T(8,128)(2,1)S(1)}, bf16[256,512]{0,1:T(8,128)(2,1)}, u32[]{:S(2)}) copy-start(bf16[256,512]{0,1:T(8,128)(2,1)} %copy-done.27) | copy-start | bytes 786436
  1019.6 57.8 %all-gather.29.cloned.1.call-start = ((), (), s32[]{:S(2)}) async-start(), calls=%async_computation.30 | async-start | bytes 2457600 | tf_op jit(solution)/shard_map/all_gather | solution.py:231
  1020.1 267.6 %all-reduce.17.cloned.1.call-start = ((), (), s32[]{:S(2)}) async-start(), calls=%async_computation.38 | async-start | bytes 2097152
  1131.3 157.9 %reduce-scatter.35.cloned.1.call-start = ((), (), s32[]{:S(2)}) async-start(), calls=%async_computation.32 | async-start | bytes 278528 | tf_op jit(solution)/shard_map/reduce_scatter | solution.py:288
  1135.3 176.4 %reduce-scatter.29.cloned.1.call-start = ((), (), s32[]{:S(2)}) async-start(), calls=%async_computation.27 | async-start | bytes 2457600 | tf_op jit(solution)/shard_map/reduce_scatter | solution.py:267
  1139.8 30.3 %copy-start.40 = (bf16[1600,768]{0,1:T(8,128)(2,1)S(1)}, bf16[1600,768]{0,1:T(8,128)(2,1)}, u32[]{:S(2)}) copy-start(bf16[1600,768]{0,1:T(8,128)(2,1)} %reshape.490) | copy-start | bytes 7372804
  1139.9 201.6 %reduce-scatter.33.cloned.1.call-start = ((), (), s32[]{:S(2)}) async-start(), calls=%async_computation.31 | async-start | bytes 2457600 | tf_op jit(solution)/shard_map/reduce_scatter | solution.py:267
  1172.8 503.4 %reduce-scatter.41.cloned.1.call-start = ((), (), s32[]{:S(2)}) async-start(), calls=%async_computation.35 | async-start | bytes 35651584 | tf_op jit(solution)/shard_map/reduce_scatter | solution.py:294
  1213.4 796.7 %reduce-scatter.39.cloned.1.call-start = ((), (), s32[]{:S(2)}) async-start(), calls=%async_computation.34 | async-start | bytes 35651584 | tf_op jit(solution)/shard_map/reduce_scatter | solution.py:291
  1278.7 868.9 %reduce-scatter.37.cloned.1.call-start = ((), (), s32[]{:S(2)}) async-start(), calls=%async_computation.33 | async-start | bytes 270336 | tf_op jit(solution)/shard_map/reduce_scatter | solution.py:303
  1283.5 57.9 %copy-start.3 = (f32[2,800,512]{2,1,0:T(8,128)S(1)}, f32[2,800,512]{2,1,0:T(8,128)}, u32[]{:S(2)}) copy-start(f32[2,800,512]{2,1,0:T(8,128)} %param.14) | copy-start | bytes 9830404
  1283.5 57.9 %copy-start.54 = (f32[800]{0:T(1024)S(1)}, f32[800]{0:T(1024)}, u32[]{:S(2)}) copy-start(f32[800]{0:T(1024)} %copy-done.53) | copy-start | bytes 9604
  1283.6 57.9 %copy-start.56 = (f32[800]{0:T(1024)S(1)}, f32[800]{0:T(1024)}, u32[]{:S(2)}) copy-start(f32[800]{0:T(1024)} %copy-done.55) | copy-start | bytes 9604
  1283.6 57.9 %copy-start.97 = (f32[512]{0:T(512)S(1)}, f32[512]{0:T(512)}, u32[]{:S(2)}) copy-start(f32[512]{0:T(512)} %copy-done.96) | copy-start | bytes 6148
  1287.7 56.4 %copy-start.91 = (f32[800]{0:T(1024)S(1)}, f32[800]{0:T(1024)}, u32[]{:S(2)}) copy-start(f32[800]{0:T(1024)} %copy-done.90) | copy-start | bytes 9604
  1287.7 56.5 %copy-start.89 = (f32[800]{0:T(1024)S(1)}, f32[800]{0:T(1024)}, u32[]{:S(2)}) copy-start(f32[800]{0:T(1024)} %copy-done.88) | copy-start | bytes 9604
  1287.7 56.5 %copy-start.77 = (f32[800]{0:T(1024)S(1)}, f32[800]{0:T(1024)}, u32[]{:S(2)}) copy-start(f32[800]{0:T(1024)} %copy-done.76) | copy-start | bytes 9604
  1287.7 56.5 %copy-start.79 = (f32[800]{0:T(1024)S(1)}, f32[800]{0:T(1024)}, u32[]{:S(2)}) copy-start(f32[800]{0:T(1024)} %copy-done.78) | copy-start | bytes 9604
  1344.1 43.5 %copy-start.85 = (f32[800]{0:T(1024)S(1)}, f32[800]{0:T(1024)}, u32[]{:S(2)}) copy-start(f32[800]{0:T(1024)} %copy-done.84) | copy-start | bytes 9604
  1344.1 43.4 %copy-start.87 = (f32[800]{0:T(1024)S(1)}, f32[800]{0:T(1024)}, u32[]{:S(2)}) copy-start(f32[800]{0:T(1024)} %copy-done.86) | copy-start | bytes 9604
  (98 other events, 489.9 us)
Sparse Core Ops, SparseCore 0:
  56.1 27.7 all-gather.10
  86.0 27.9 all-gather.18
  146.6 24.4 reduce-scatter.18
  190.6 24.4 reduce-scatter.22
  221.7 29.6 all-gather.20
  252.8 29.5 all-gather.12
  284.0 168.2 all-gather.14
  453.8 168.0 all-gather.16
  624.0 27.8 all-gather.26
  653.3 27.9 all-gather.22
  690.6 13.3 reduce-scatter.44
  844.5 13.3 reduce-scatter.42
  860.1 26.8 reduce-scatter.26
  923.1 26.7 reduce-scatter.30
  953.3 26.7 reduce-scatter.24
  983.1 26.7 reduce-scatter.20
  1019.7 27.7 all-gather.24
  1049.4 27.9 all-gather.28
  1131.5 93.7 all-reduce.16
  1228.6 54.8 reduce-scatter.34
  1285.7 25.9 reduce-scatter.28
  1314.5 26.8 reduce-scatter.32
  1345.7 330.5 reduce-scatter.40
  1680.4 329.6 reduce-scatter.38
  2012.8 134.7 reduce-scatter.36
where the time goes:
time: 2160 us; the launch traced here: 2150 us
  waiting for transfers between devices  1100 us (51%)
  matrix products  465 us (22%)
  local copies, waits for them, and re-layouts  293 us (14%)
  blocking collectives  194 us (9%)
  other arithmetic  82 us (4%)
    reduce_scatter x1, waiting for transfers between devices, per_device(): lax.psum_scatter(first_acc.astype(jnp.bfloat16), 'dp', scatter_dimension=...  330 us
    reduce_scatter x1, waiting for transfers between devices, per_device(): lax.psum_scatter(second_acc.astype(jnp.bfloat16), 'dp', scatter_dimension...  281 us
    all_gather x1, waiting for transfers between devices, current_weights(): lax.all_gather(expert_out, 'dp', axis=2, tiled=True)  148 us
    reduce_scatter x1, waiting for transfers between devices, per_device(): lax.psum_scatter(router_acc, ('dp', 'tensor'), scatter_dimension=0, tiled...  133 us
    all_gather x1, waiting for transfers between devices, current_weights(): lax.all_gather(expert_in, 'dp', axis=1, tiled=True)  87.7 us
    unnamed x2, blocking collectives  81.4 us
    dot_general x2, matrix products, per_device(): jnp.einsum('ecf,ecd->efd', hidden, result_grad, preferred_element_type=jn...  70.7 us
    all_gather x1, blocking collectives, per_device(): lax.all_gather(router_weight, ('dp', 'tensor'), axis=0, tiled=True)  69.3 us
  transfers between devices with their start and end apart: 25, of which 11 were waited for; matrix products, arithmetic and copies ran while one was open for 35% of the time, Pallas kernels for 0%

commit v1 on v0

--- a/solution.py
+++ b/solution.py
@@ -8,6 +8,27 @@
 EPSILON = 1e-06
 FIRST_DIMS = (((0,), (0,)), ((), ()))
 LAST_DIMS = (((1,), (1,)), ((), ()))
+
+
+def gather_around(x, axis, dim):
+    size, index, span = (lax.axis_size(axis), lax.axis_index(axis), x.shape[dim])
+    right = [(i, (i + 1) % size) for i in range(size)]
+    downward = [(i, (i - 1) % size) for i in range(size)]
+    out = jnp.zeros((*x.shape[:dim], size * span, *x.shape[dim + 1 :]), x.dtype)
+    out = lax.dynamic_update_slice_in_dim(out, x, index * span, axis=dim)
+    from_left = from_right = x
+    half = size // 2
+    for step in range(1, half + 1):
+        from_left = lax.ppermute(from_left, axis, right)
+        out = lax.dynamic_update_slice_in_dim(
+            out, from_left, (index - step) % size * span, axis=dim
+        )
+        if step < size - half:
+            from_right = lax.ppermute(from_right, axis, downward)
+            out = lax.dynamic_update_slice_in_dim(
+                out, from_right, (index + step) % size * span, axis=dim
+            )
+    return out
 
 
 def norm_rows(values, gain, offset):
@@ -71,7 +92,7 @@
             fetch_attention(),
             (
                 lax.all_gather(expert_in, "dp", axis=1, tiled=True),
-                lax.all_gather(expert_out, "dp", axis=2, tiled=True),
+                gather_around(expert_out, "dp", 2),
             ),
         )
 

time: 2160 us -> 3910 us (1.81); the launches traced: 2150 us -> 3860 us
  local copies, waits for them, and re-layouts: 293 us -> 1830 us
  starting transfers between devices: 1.58 us -> 338 us
  waiting for transfers between devices: 1100 us -> 918 us
    dynamic_update_slice x0 -> x16, local copies, waits for them, and re-layouts: none -> 1410 us  [the longest x8 700 us: gather_around(): lax.dynamic_update_slice_in_dim(out, from_left, (index - step) % size * s...]
    ppermute x0 -> x15, starting transfers between devices: none -> 336 us  [the longest x8 327 us: gather_around(): from_left = lax.ppermute(from_left, axis, right)]
    all_gather x1 -> x0, waiting for transfers between devices: 148 us -> none  [current_weights(): lax.all_gather(expert_out, 'dp', axis=2, tiled=True)]
    ppermute x0 -> x15, local copies, waits for them, and re-layouts: none -> 115 us  [the longest x8 62.7 us: gather_around(): from_left = lax.ppermute(from_left, axis, right)]
    all_gather x1, waiting for transfers between devices: 87.7 us -> 0.01 us  [current_weights(): lax.all_gather(expert_in, 'dp', axis=1, tiled=True)]
    ppermute x0 -> x15, waiting for transfers between devices: none -> 49.3 us  [the longest x8 38.8 us: gather_around(): from_left = lax.ppermute(from_left, axis, right)]
    reduce_scatter x1, waiting for transfers between devices: 281 us -> 330 us  [per_device(): lax.psum_scatter(second_acc.astype(jnp.bfloat16), 'dp', scatter_dimension...]
    reduce_scatter x1, waiting for transfers between devices: 330 us -> 281 us  [per_device(): lax.psum_scatter(first_acc.astype(jnp.bfloat16), 'dp', scatter_dimension=...]
  transfers between devices with their start and end apart: 25 -> 39, of which waited for: 11 -> 15; matrix products, arithmetic and copies ran while one was open for 35% -> 60% of each run, Pallas kernels for 0% -> 0%
where the time goes in v1:
time: 3910 us; the launch traced here: 3860 us
  local copies, waits for them, and re-layouts  1830 us (47%)
  waiting for transfers between devices  918 us (23%)
  matrix products  464 us (12%)
  starting transfers between devices  338 us (9%)
  blocking collectives  210 us (5%)
  other arithmetic  82.4 us (2%)
    dynamic_update_slice x8, local copies, waits for them, and re-layouts, gather_around(): lax.dynamic_update_slice_in_dim(out, from_left, (index - step) % size * s...  700 us
    dynamic_update_slice x7, local copies, waits for them, and re-layouts, gather_around(): lax.dynamic_update_slice_in_dim(out, from_right, (index + step) % size *...  629 us
    reduce_scatter x1, waiting for transfers between devices, per_device(): lax.psum_scatter(second_acc.astype(jnp.bfloat16), 'dp', scatter_dimension...  330 us
    ppermute x8, starting transfers between devices, gather_around(): from_left = lax.ppermute(from_left, axis, right)  327 us
    reduce_scatter x1, waiting for transfers between devices, per_device(): lax.psum_scatter(first_acc.astype(jnp.bfloat16), 'dp', scatter_dimension=...  281 us
    reduce_scatter x1, waiting for transfers between devices, per_device(): lax.psum_scatter(router_acc, ('dp', 'tensor'), scatter_dimension=0, tiled...  133 us
    all_gather x1, blocking collectives, per_device(): lax.all_gather(router_weight, ('dp', 'tensor'), axis=0, tiled=True)  85.6 us
    unnamed x2, blocking collectives  81.4 us
  transfers between devices with their start and end apart: 39, of which 15 were waited for; matrix products, arithmetic and copies ran while one was open for 60% of the time, Pallas kernels for 0%

profile of v1, /device:TPU:0, one launch (start us, length us, event | category | flops | bytes accessed | tf_op | source)
XLA Modules:
  0.0 3864.5 jit_solution(1955664422981135792)
XLA Ops:
  12.3 42.0 %all-reduce.14 = (f32[512]{0:T(512)S(1)}, f32[512]{0:T(512)S(1)}, f32[512]{0:T(512)S(1)}, f32[512]{0:T(512)S(1)}) all-reduce(f32[512]{0:T(512)S(1)} %dynamic-update-slice.1, f32[512]{0:T(512)S(1)} %dynamic-update-slice, f32[512]{0:T(512)S(1)} %dynamic-update-slice.3, ...), channel_id=1, replica_groups=mesh['dp'=16,'tensor'=2] {'dp','tensor'}, use_global_device_ids=true, to_apply=%add.5 | all-reduce | flops 2048 | bytes 16384
  56.8 24.6 all_gather.60
  83.8 18.6 all_gather.61
  190.3 24.5 reduce-scatter.23.cloned.1.call-done
  226.9 24.0 collective-permute-done
  251.0 18.9 collective-permute-start.2
  279.2 102.0 %collective-permute-start.4 = (bf16[32,1024,32]{1,2,0:T(8,128)(2,1)S(1)}, bf16[32,1024,32]{1,2,0:T(8,128)(2,1)}, u32[]{:S(2)}, u32[]{:S(2)}) collective-permute-start(bf16[32,1024,32]{1,2,0:T(8,128)(2,1)S(1)} %collective-permute-done.2), channel_id=1, source_target_pairs={{0,2},{2,4},{4,6},{6,8},{8,10},{10,12},{12,14},{14,16},{16,18},{18... | collective-permute-start | bytes 6291464 | tf_op jit(solution)/shard_map/ppermute | solution.py:22
  385.2 89.2 %collective-permute-start.6 = (bf16[32,1024,32]{1,2,0:T(8,128)(2,1)}, bf16[32,1024,32]{1,2,0:T(8,128)(2,1)}, u32[]{:S(2)}, u32[]{:S(2)}) collective-permute-start(bf16[32,1024,32]{1,2,0:T(8,128)(2,1)} %collective-permute-done.4), channel_id=1, source_target_pairs={{0,2},{2,4},{4,6},{6,8},{8,10},{10,12},{12,14},{14,16},{16,18},{18... | collective-permute-start | bytes 6291464 | tf_op jit(solution)/shard_map/ppermute | solution.py:22
  478.5 67.4 %collective-permute-start.8 = (bf16[32,1024,32]{1,2,0:T(8,128)(2,1)}, bf16[32,1024,32]{1,2,0:T(8,128)(2,1)}, u32[]{:S(2)}, u32[]{:S(2)}) collective-permute-start(bf16[32,1024,32]{1,2,0:T(8,128)(2,1)} %collective-permute-done.6), channel_id=1, source_target_pairs={{0,2},{2,4},{4,6},{6,8},{8,10},{10,12},{12,14},{14,16},{16,18},{18... | collective-permute-start | bytes 6291464 | tf_op jit(solution)/shard_map/ppermute | solution.py:22
  569.8 78.8 %dynamic_update_slice.32 = bf16[32,1024,512]{2,1,0:T(8,128)(2,1)} dynamic-update-slice(bf16[32,1024,512]{2,1,0:T(8,128)(2,1)} %broadcast.465, bf16[32,1024,32]{2,1,0:T(8,128)(2,1)} %copy.301, s32[]{:T(128)} %constant.236.clone.1, s32[]{:T(128)} %constant.236.clone.1, s32[]{:T(128)S(6)} %select_n.395) | dynamic-update-slice | bytes 4194308 | tf_op jit(solution)/shard_map/dynamic_update_slice | solution.py:18
  667.1 85.6 %all_gather.65 = f32[512,32]{1,0:T(8,128)S(1)} all-gather(f32[16,32]{1,0:T(8,128)S(1)} %copy-done.110), channel_id=1, replica_groups=mesh['dp'=16,'tensor'=2] {'dp','tensor'}, dimensions={0}, use_global_device_ids=true | all-gather | bytes 67584 | tf_op jit(solution)/shard_map/all_gather | solution.py:69
  761.2 90.0 %dynamic_update_slice.33 = bf16[32,1024,512]{2,1,0:T(8,128)(2,1)} dynamic-update-slice(bf16[32,1024,512]{2,1,0:T(8,128)(2,1)} %dynamic_update_slice.32, bf16[32,1024,32]{2,1,0:T(8,128)(2,1)} %copy.302, s32[]{:T(128)} %constant.236.clone.1, s32[]{:T(128)} %constant.236.clone.1, s32[]{:T(128)S(6)} %select_n.397) | dynamic-update-slice | bytes 4194308 | tf_op jit(solution)/shard_map/dynamic_update_slice | solution.py:23
  859.0 91.7 %dynamic_update_slice.34 = bf16[32,1024,512]{2,1,0:T(8,128)(2,1)} dynamic-update-slice(bf16[32,1024,512]{2,1,0:T(8,128)(2,1)} %dynamic_update_slice.33, bf16[32,1024,32]{2,1,0:T(8,128)(2,1)} %copy.303, s32[]{:T(128)} %constant.236.clone.1, s32[]{:T(128)} %constant.236.clone.1, s32[]{:T(128)S(6)} %select_n.399) | dynamic-update-slice | bytes 4194308 | tf_op jit(solution)/shard_map/dynamic_update_slice | solution.py:28
  958.4 90.0 %dynamic_update_slice.35 = bf16[32,1024,512]{2,1,0:T(8,128)(2,1)} dynamic-update-slice(bf16[32,1024,512]{2,1,0:T(8,128)(2,1)} %dynamic_update_slice.34, bf16[32,1024,32]{2,1,0:T(8,128)(2,1)} %copy.304, s32[]{:T(128)} %constant.236.clone.1, s32[]{:T(128)} %constant.236.clone.1, s32[]{:T(128)S(6)} %select_n.401) | dynamic-update-slice | bytes 4194308 | tf_op jit(solution)/shard_map/dynamic_update_slice | solution.py:23
  1056.2 91.7 %dynamic_update_slice.36 = bf16[32,1024,512]{2,1,0:T(8,128)(2,1)} dynamic-update-slice(bf16[32,1024,512]{2,1,0:T(8,128)(2,1)} %dynamic_update_slice.35, bf16[32,1024,32]{2,1,0:T(8,128)(2,1)} %copy.305, s32[]{:T(128)} %constant.236.clone.1, s32[]{:T(128)} %constant.236.clone.1, s32[]{:T(128)S(6)} %select_n.403) | dynamic-update-slice | bytes 4194308 | tf_op jit(solution)/shard_map/dynamic_update_slice | solution.py:28
  1155.7 90.0 %dynamic_update_slice.37 = bf16[32,1024,512]{2,1,0:T(8,128)(2,1)} dynamic-update-slice(bf16[32,1024,512]{2,1,0:T(8,128)(2,1)} %dynamic_update_slice.36, bf16[32,1024,32]{2,1,0:T(8,128)(2,1)} %copy.306, s32[]{:T(128)} %constant.236.clone.1, s32[]{:T(128)} %constant.236.clone.1, s32[]{:T(128)S(6)} %select_n.405) | dynamic-update-slice | bytes 4194308 | tf_op jit(solution)/shard_map/dynamic_update_slice | solution.py:23
  1253.5 91.7 %dynamic_update_slice.38 = bf16[32,1024,512]{2,1,0:T(8,128)(2,1)} dynamic-update-slice(bf16[32,1024,512]{2,1,0:T(8,128)(2,1)} %dynamic_update_slice.37, bf16[32,1024,32]{2,1,0:T(8,128)(2,1)} %copy.307, s32[]{:T(128)} %constant.236.clone.1, s32[]{:T(128)} %constant.236.clone.1, s32[]{:T(128)S(6)} %select_n.407) | dynamic-update-slice | bytes 4194308 | tf_op jit(solution)/shard_map/dynamic_update_slice | solution.py:28
  1380.8 32.5 collective-permute-start.14
  1465.8 76.5 %dynamic_update_slice.39 = bf16[32,1024,512]{2,1,0:T(8,128)(2,1)} dynamic-update-slice(bf16[32,1024,512]{2,1,0:T(8,128)(2,1)} %dynamic_update_slice.38, bf16[32,1024,32]{2,1,0:T(8,128)(2,1)} %copy.308, s32[]{:T(128)} %constant.236.clone.1, s32[]{:T(128)} %constant.236.clone.1, s32[]{:T(128)S(6)} %select_n.409) | dynamic-update-slice | bytes 4194308 | tf_op jit(solution)/shard_map/dynamic_update_slice | solution.py:23
  1548.2 78.6 %dynamic_update_slice.40 = bf16[32,1024,512]{2,1,0:T(8,128)(2,1)} dynamic-update-slice(bf16[32,1024,512]{2,1,0:T(8,128)(2,1)} %dynamic_update_slice.39, bf16[32,1024,32]{2,1,0:T(8,128)(2,1)} %copy.309, s32[]{:T(128)} %constant.236.clone.1, s32[]{:T(128)} %constant.236.clone.1, s32[]{:T(128)S(6)} %select_n.411) | dynamic-update-slice | bytes 4194308 | tf_op jit(solution)/shard_map/dynamic_update_slice | solution.py:28
  1634.6 91.6 %dynamic_update_slice.41 = bf16[32,1024,512]{2,1,0:T(8,128)(2,1)} dynamic-update-slice(bf16[32,1024,512]{2,1,0:T(8,128)(2,1)} %dynamic_update_slice.40, bf16[32,1024,32]{2,1,0:T(8,128)(2,1)} %copy.310, s32[]{:T(128)} %constant.236.clone.1, s32[]{:T(128)} %constant.236.clone.1, s32[]{:T(128)S(6)} %select_n.413) | dynamic-update-slice | bytes 4194308 | tf_op jit(solution)/shard_map/dynamic_update_slice | solution.py:23
  1734.0 91.6 %dynamic_update_slice.42 = bf16[32,1024,512]{2,1,0:T(8,128)(2,1)} dynamic-update-slice(bf16[32,1024,512]{2,1,0:T(8,128)(2,1)} %dynamic_update_slice.41, bf16[32,1024,32]{2,1,0:T(8,128)(2,1)} %copy.311, s32[]{:T(128)} %constant.236.clone.1, s32[]{:T(128)} %constant.236.clone.1, s32[]{:T(128)S(6)} %select_n.415) | dynamic-update-slice | bytes 4194308 | tf_op jit(solution)/shard_map/dynamic_update_slice | solution.py:28
  1833.4 91.6 %dynamic_update_slice.43 = bf16[32,1024,512]{2,1,0:T(8,128)(2,1)} dynamic-update-slice(bf16[32,1024,512]{2,1,0:T(8,128)(2,1)} %dynamic_update_slice.42, bf16[32,1024,32]{2,1,0:T(8,128)(2,1)} %copy.312, s32[]{:T(128)} %constant.236.clone.1, s32[]{:T(128)} %constant.236.clone.1, s32[]{:T(128)S(6)} %select_n.417) | dynamic-update-slice | bytes 4194308 | tf_op jit(solution)/shard_map/dynamic_update_slice | solution.py:23
  1932.9 91.6 %dynamic_update_slice.44 = bf16[32,1024,512]{2,1,0:T(8,128)(2,1)} dynamic-update-slice(bf16[32,1024,512]{2,1,0:T(8,128)(2,1)} %dynamic_update_slice.43, bf16[32,1024,32]{2,1,0:T(8,128)(2,1)} %copy.313, s32[]{:T(128)} %constant.236.clone.1, s32[]{:T(128)} %constant.236.clone.1, s32[]{:T(128)S(6)} %select_n.419) | dynamic-update-slice | bytes 4194308 | tf_op jit(solution)/shard_map/dynamic_update_slice | solution.py:28
  2032.3 91.6 %dynamic_update_slice.45 = bf16[32,1024,512]{2,1,0:T(8,128)(2,1)} dynamic-update-slice(bf16[32,1024,512]{2,1,0:T(8,128)(2,1)} %dynamic_update_slice.44, bf16[32,1024,32]{2,1,0:T(8,128)(2,1)} %copy.314, s32[]{:T(128)} %constant.236.clone.1, s32[]{:T(128)} %constant.236.clone.1, s32[]{:T(128)S(6)} %select_n.421) | dynamic-update-slice | bytes 4194308 | tf_op jit(solution)/shard_map/dynamic_update_slice | solution.py:23
  2131.7 91.6 %dynamic_update_slice.46 = bf16[32,1024,512]{2,1,0:T(8,128)(2,1)} dynamic-update-slice(bf16[32,1024,512]{2,1,0:T(8,128)(2,1)} %dynamic_update_slice.45, bf16[32,1024,32]{2,1,0:T(8,128)(2,1)} %copy.315, s32[]{:T(128)} %constant.236.clone.1, s32[]{:T(128)} %constant.236.clone.1, s32[]{:T(128)S(6)} %select_n.423) | dynamic-update-slice | bytes 4194308 | tf_op jit(solution)/shard_map/dynamic_update_slice | solution.py:28
  2231.2 78.5 %dynamic_update_slice.47 = bf16[32,1024,512]{2,1,0:T(8,128)(2,1)} dynamic-update-slice(bf16[32,1024,512]{2,1,0:T(8,128)(2,1)} %dynamic_update_slice.46, bf16[32,1024,32]{2,1,0:T(8,128)(2,1)} %copy.316, s32[]{:T(128)} %constant.236.clone.1, s32[]{:T(128)} %constant.236.clone.1, s32[]{:T(128)S(6)} %select_n.425) | dynamic-update-slice | bytes 4194308 | tf_op jit(solution)/shard_map/dynamic_update_slice | solution.py:23
  2309.7 20.1 fusion.144
  2329.8 21.2 fusion.129
  2369.0 24.3 fusion.16
  2393.3 19.2 gather_fusion.6
  2414.1 20.1 fusion.145
  2434.2 21.1 fusion.130
  2473.8 24.3 fusion.23
  2498.1 21.0 fusion.146
  2544.9 19.1 gather_fusion.9
  2569.5 21.2 fusion.147
  2728.3 29.2 all-gather.22.cloned.1.call-done
  2849.7 27.9 fusion.150
  2880.3 38.0 add_convert_fusion.1
  2918.4 30.0 fusion.128
  2948.4 40.3 %add_convert_fusion = bf16[32,1024,512]{1,2,0:T(8,128)(2,1)} fusion(f32[32,1024,512]{1,2,0:T(8,128)} %fusion.128, bf16[32,120,512]{2,1,0:T(8,128)(2,1)} %bitcast.287, f32[32,120,1024]{2,1,0:T(8,128)} %fusion.145), kind=kOutput, calls=%fused_computation.12 | convolution fusion | flops 4095475712 | bytes 120324096 | tf_op jit(solution)/shard_map/ecf,ecd->efd/dot_general | solution.py:215
  3000.8 20.7 reduce-scatter.29.cloned.1.call-done
  3021.5 29.7 reduce-scatter.33.cloned.1.call-done
  3055.7 39.4 %all-reduce.13 = (f32[512]{0:T(512)S(1)}, f32[512]{0:T(512)S(1)}, f32[512]{0:T(512)S(1)}, f32[512]{0:T(512)S(1)}) all-reduce(f32[512]{0:T(512)S(1)} %add.647, f32[512]{0:T(512)S(1)} %add.648, f32[512]{0:T(512)S(1)} %add.651, f32[512]{0:T(512)S(1)} %add.652), channel_id=12, replica_groups=mesh['dp'=16,'tensor'=2] {'dp','tensor'}, use_global_device_ids=true, to_apply=%region_52.53.clone | all-reduce | flops 2048 | bytes 16384
  3104.9 281.1 %reduce-scatter.39.cloned.1.call-done = bf16[32,32,1024]{2,1,0:T(8,128)(2,1)} async-done(((bf16[32,512,1024]{2,1,0:T(8,128)(2,1)}), bf16[32,32,1024]{2,1,0:T(8,128)(2,1)}) %reduce-scatter.39.cloned.1.call-update) | async-done | bytes 2097168 | tf_op jit(solution)/shard_map/reduce_scatter | solution.py:312
  3390.1 329.9 %reduce-scatter.41.cloned.1.call-done = bf16[32,1024,32]{1,2,0:T(8,128)(2,1)} async-done(((bf16[32,1024,512]{1,2,0:T(8,128)(2,1)}), bf16[32,1024,32]{1,2,0:T(8,128)(2,1)}) %reduce-scatter.41.cloned.1.call-update) | async-done | bytes 2097168 | tf_op jit(solution)/shard_map/reduce_scatter | solution.py:315
  3724.1 133.3 %reduce-scatter.37.cloned.1.call-done = f32[16,32]{1,0:T(8,128)} async-done(((f32[512,32]{1,0:T(8,128)}), f32[16,32]{1,0:T(8,128)}) %reduce-scatter.37.cloned.1.call-update) | async-done | bytes 2064 | tf_op jit(solution)/shard_map/reduce_scatter | solution.py:324
  (549 shorter events, 699.5 us)
Async XLA Ops:
  7.2 95.1 %all-gather.10.cloned.1.call-start = ((), (), s32[]{:S(2)}) async-start(), calls=%async_computation.14 | async-start | bytes 2457600 | tf_op jit(solution)/shard_map/all_gather | solution.py:130
  54.3 164.6 %copy-start.103 = (f32[512]{0:T(512)}, f32[512]{0:T(512)S(1)}, u32[]{:S(2)}) copy-start(f32[512]{0:T(512)S(1)} %get-tuple-element.101) | copy-start | bytes 6148
  56.0 90.5 %all-gather.16.cloned.1.call-start = ((), (), s32[]{:S(2)}) async-start(), calls=%async_computation.19 | async-start | bytes 2457600 | tf_op jit(solution)/shard_map/all_gather | solution.py:130
  56.8 133.5 %reduce-scatter.19.cloned.1.call-start = ((), (), s32[]{:S(2)}) async-start(), calls=%async_computation.15 | async-start | bytes 2457600 | tf_op jit(solution)/shard_map/reduce_scatter | solution.py:149
  102.3 84.9 %copy-start.27 = (bf16[256,512]{0,1:T(8,128)(2,1)}, bf16[256,512]{0,1:T(8,128)(2,1)S(1)}, u32[]{:S(2)}) copy-start(bf16[256,512]{0,1:T(8,128)(2,1)S(1)} %all_gather.61) | copy-start | bytes 786436
  146.2 68.6 %reduce-scatter.23.cloned.1.call-start = ((), (), s32[]{:S(2)}) async-start(), calls=%async_computation.20 | async-start | bytes 2457600 | tf_op jit(solution)/shard_map/reduce_scatter | solution.py:149
  190.2 1154.9 %all-gather.12.cloned.1.call-start = ((), (), s32[]{:S(2)}) async-start(), calls=%async_computation.16 | async-start | bytes 2457600 | tf_op jit(solution)/shard_map/all_gather | solution.py:156
  218.9 255.5 %copy-start.10 = (f32[2,800,512]{2,1,0:T(8,128)S(1)}, f32[2,800,512]{2,1,0:T(8,128)}, u32[]{:S(2)}) copy-start(f32[2,800,512]{2,1,0:T(8,128)} %param.27) | copy-start | bytes 9830404
  220.6 1128.4 %all-gather.18.cloned.1.call-start = ((), (), s32[]{:S(2)}) async-start(), calls=%async_computation.21 | async-start | bytes 2457600 | tf_op jit(solution)/shard_map/all_gather | solution.py:156
  221.2 2088.5 %all-gather.14.cloned.1.call-start = ((), (), s32[]{:S(2)}) async-start(), calls=%async_computation.17 | async-start | bytes 35651584 | tf_op jit(solution)/shard_map/all_gather | solution.py:94
  221.9 2129.2 %all-gather.20.cloned.1.call-start = ((), (), s32[]{:S(2)}) async-start(), calls=%async_computation.23 | async-start | bytes 2457600 | tf_op jit(solution)/shard_map/all_gather | solution.py:198
  222.0 29.0 collective-permute-start
  222.5 47.3 %collective-permute-start.1 = (bf16[32,1024,32]{1,2,0:T(8,128)(2,1)}, bf16[32,1024,32]{1,2,0:T(8,128)(2,1)S(1)}, u32[]{:S(2)}, u32[]{:S(2)}) collective-permute-start(bf16[32,1024,32]{1,2,0:T(8,128)(2,1)} %param.26), channel_id=1, source_target_pairs={{0,30},{2,0},{4,2},{6,4},{8,6},{10,8},{12,10},{14,12},{16,14},{18,... | collective-permute-start | bytes 6291464 | tf_op jit(solution)/shard_map/ppermute | solution.py:27
  251.0 134.2 %copy-start.43 = (bf16[32,1024,32]{1,2,0:T(8,128)(2,1)}, bf16[32,1024,32]{1,2,0:T(8,128)(2,1)S(1)}, u32[]{:S(2)}) copy-start(bf16[32,1024,32]{1,2,0:T(8,128)(2,1)S(1)} %collective-permute-done) | copy-start | bytes 6291460
  251.0 28.3 collective-permute-start.2
  271.2 110.1 %collective-permute-start.3 = (bf16[32,1024,32]{1,2,0:T(8,128)(2,1)S(1)}, bf16[32,1024,32]{1,2,0:T(8,128)(2,1)}, u32[]{:S(2)}, u32[]{:S(2)}) collective-permute-start(bf16[32,1024,32]{1,2,0:T(8,128)(2,1)S(1)} %collective-permute-done.1), channel_id=1, source_target_pairs={{0,30},{2,0},{4,2},{6,4},{8,6},{10,8},{12,10},{14,12},{16,14},{18,... | collective-permute-start | bytes 6291464 | tf_op jit(solution)/shard_map/ppermute | solution.py:27
  279.2 102.0 %copy-start.42 = (bf16[32,1024,32]{1,2,0:T(8,128)(2,1)}, bf16[32,1024,32]{1,2,0:T(8,128)(2,1)S(1)}, u32[]{:S(2)}) copy-start(bf16[32,1024,32]{1,2,0:T(8,128)(2,1)S(1)} %collective-permute-done.2) | copy-start | bytes 6291460
  279.2 105.9 %collective-permute-start.4 = (bf16[32,1024,32]{1,2,0:T(8,128)(2,1)S(1)}, bf16[32,1024,32]{1,2,0:T(8,128)(2,1)}, u32[]{:S(2)}, u32[]{:S(2)}) collective-permute-start(bf16[32,1024,32]{1,2,0:T(8,128)(2,1)S(1)} %collective-permute-done.2), channel_id=1, source_target_pairs={{0,2},{2,4},{4,6},{6,8},{8,10},{10,12},{12,14},{14,16},{16,18},{18... | collective-permute-start | bytes 6291464 | tf_op jit(solution)/shard_map/ppermute | solution.py:22
  381.3 94.6 %collective-permute-start.5 = (bf16[32,1024,32]{1,2,0:T(8,128)(2,1)}, bf16[32,1024,32]{1,2,0:T(8,128)(2,1)}, u32[]{:S(2)}, u32[]{:S(2)}) collective-permute-start(bf16[32,1024,32]{1,2,0:T(8,128)(2,1)} %collective-permute-done.3), channel_id=1, source_target_pairs={{0,30},{2,0},{4,2},{6,4},{8,6},{10,8},{12,10},{14,12},{16,14},{18,... | collective-permute-start | bytes 6291464 | tf_op jit(solution)/shard_map/ppermute | solution.py:27
  385.2 93.3 %collective-permute-start.6 = (bf16[32,1024,32]{1,2,0:T(8,128)(2,1)}, bf16[32,1024,32]{1,2,0:T(8,128)(2,1)}, u32[]{:S(2)}, u32[]{:S(2)}) collective-permute-start(bf16[32,1024,32]{1,2,0:T(8,128)(2,1)} %collective-permute-done.4), channel_id=1, source_target_pairs={{0,2},{2,4},{4,6},{6,8},{8,10},{10,12},{12,14},{14,16},{16,18},{18... | collective-permute-start | bytes 6291464 | tf_op jit(solution)/shard_map/ppermute | solution.py:22
  475.8 1980.0 %all-gather.24.cloned.1.call-start = ((), (), s32[]{:S(2)}) async-start(), calls=%async_computation.27 | async-start | bytes 2457600 | tf_op jit(solution)/shard_map/all_gather | solution.py:198
  475.9 175.4 %collective-permute-start.7 = (bf16[32,1024,32]{1,2,0:T(8,128)(2,1)}, bf16[32,1024,32]{1,2,0:T(8,128)(2,1)S(1)}, u32[]{:S(2)}, u32[]{:S(2)}) collective-permute-start(bf16[32,1024,32]{1,2,0:T(8,128)(2,1)} %collective-permute-done.5), channel_id=1, source_target_pairs={{0,30},{2,0},{4,2},{6,4},{8,6},{10,8},{12,10},{14,12},{16,14},{18,... | collective-permute-start | bytes 6291464 | tf_op jit(solution)/shard_map/ppermute | solution.py:27
  478.5 172.8 %collective-permute-start.8 = (bf16[32,1024,32]{1,2,0:T(8,128)(2,1)}, bf16[32,1024,32]{1,2,0:T(8,128)(2,1)}, u32[]{:S(2)}, u32[]{:S(2)}) collective-permute-start(bf16[32,1024,32]{1,2,0:T(8,128)(2,1)} %collective-permute-done.6), channel_id=1, source_target_pairs={{0,2},{2,4},{4,6},{6,8},{8,10},{10,12},{12,14},{14,16},{16,18},{18... | collective-permute-start | bytes 6291464 | tf_op jit(solution)/shard_map/ppermute | solution.py:22
  546.0 2144.5 %reduce-scatter.43.cloned.1.call-start = ((), (), s32[]{:S(2)}) async-start(), calls=%async_computation.35 | async-start | bytes 614400
  569.8 97.2 %copy-start.110 = (f32[16,32]{1,0:T(8,128)S(1)}, f32[16,32]{1,0:T(8,128)}, u32[]{:S(2)}) copy-start(f32[16,32]{1,0:T(8,128)} %param.24) | copy-start | bytes 6148
  650.7 795.1 %copy-start.111 = (s32[1600]{0:T(1024)}, s32[1600]{0:T(1024)S(1)}, u32[]{:S(2)}) copy-start(s32[1600]{0:T(1024)S(1)} %get-tuple-element.92) | copy-start | bytes 19204
  650.7 795.1 %copy-start.113 = (s32[1600]{0:T(1024)}, s32[1600]{0:T(1024)S(1)}, u32[]{:S(2)}) copy-start(s32[1600]{0:T(1024)S(1)} %get-tuple-element.93) | copy-start | bytes 19204
  651.3 700.7 %collective-permute-start.9 = (bf16[32,1024,32]{1,2,0:T(8,128)(2,1)S(1)}, bf16[32,1024,32]{1,2,0:T(8,128)(2,1)}, u32[]{:S(2)}, u32[]{:S(2)}) collective-permute-start(bf16[32,1024,32]{1,2,0:T(8,128)(2,1)S(1)} %collective-permute-done.7), channel_id=1, source_target_pairs={{0,30},{2,0},{4,2},{6,4},{8,6},{10,8},{12,10},{14,12},{16,14},{18,... | collective-permute-start | bytes 6291464 | tf_op jit(solution)/shard_map/ppermute | solution.py:27
  651.3 700.7 %collective-permute-start.10 = (bf16[32,1024,32]{1,2,0:T(8,128)(2,1)}, bf16[32,1024,32]{1,2,0:T(8,128)(2,1)}, u32[]{:S(2)}, u32[]{:S(2)}) collective-permute-start(bf16[32,1024,32]{1,2,0:T(8,128)(2,1)} %collective-permute-done.8), channel_id=1, source_target_pairs={{0,2},{2,4},{4,6},{6,8},{8,10},{10,12},{12,14},{14,16},{16,18},{18... | collective-permute-start | bytes 6291464 | tf_op jit(solution)/shard_map/ppermute | solution.py:22
  752.7 596.3 %copy-start.16 = (f32[512,32]{1,0:T(8,128)}, f32[512,32]{1,0:T(8,128)S(1)}, u32[]{:S(2)}) copy-start(f32[512,32]{1,0:T(8,128)S(1)} %all_gather.65) | copy-start | bytes 196612
  1352.0 23.9 collective-permute-start.11
  1352.0 28.8 collective-permute-start.12
  1375.9 748.0 %collective-permute-start.13 = (bf16[32,1024,32]{1,2,0:T(8,128)(2,1)}, bf16[32,1024,32]{1,2,0:T(8,128)(2,1)}, u32[]{:S(2)}, u32[]{:S(2)}) collective-permute-start(bf16[32,1024,32]{1,2,0:T(8,128)(2,1)} %collective-permute-done.11), channel_id=1, source_target_pairs={{0,30},{2,0},{4,2},{6,4},{8,6},{10,8},{12,10},{14,12},{16,14},{18,... | collective-permute-start | bytes 6291464 | tf_op jit(solution)/shard_map/ppermute | solution.py:27
  1380.8 842.5 %collective-permute-start.14 = (bf16[32,1024,32]{1,2,0:T(8,128)(2,1)}, bf16[32,1024,32]{1,2,0:T(8,128)(2,1)}, u32[]{:S(2)}, u32[]{:S(2)}) collective-permute-start(bf16[32,1024,32]{1,2,0:T(8,128)(2,1)} %collective-permute-done.12), channel_id=1, source_target_pairs={{0,2},{2,4},{4,6},{6,8},{8,10},{10,12},{12,14},{14,16},{16,18},{18... | collective-permute-start | bytes 6291464 | tf_op jit(solution)/shard_map/ppermute | solution.py:22
  2455.3 238.0 %reduce-scatter.45.cloned.1.call-start = ((), (), s32[]{:S(2)}) async-start(), calls=%async_computation.36 | async-start | bytes 614400
  2565.7 134.7 %reduce-scatter.27.cloned.1.call-start = ((), (), s32[]{:S(2)}) async-start(), calls=%async_computation.24 | async-start | bytes 2457600 | tf_op jit(solution)/shard_map/reduce_scatter | solution.py:228
  2569.5 134.9 %reduce-scatter.31.cloned.1.call-start = ((), (), s32[]{:S(2)}) async-start(), calls=%async_computation.28 | async-start | bytes 2457600 | tf_op jit(solution)/shard_map/reduce_scatter | solution.py:228
  2620.9 89.5 %reduce-scatter.25.cloned.1.call-start = ((), (), s32[]{:S(2)}) async-start(), calls=%async_computation.22 | async-start | bytes 2457600 | tf_op jit(solution)/shard_map/reduce_scatter | solution.py:185
  2651.0 69.0 %reduce-scatter.21.cloned.1.call-start = ((), (), s32[]{:S(2)}) async-start(), calls=%async_computation.18 | async-start | bytes 2457600 | tf_op jit(solution)/shard_map/reduce_scatter | solution.py:185
  2681.7 75.7 %all-gather.22.cloned.1.call-start = ((), (), s32[]{:S(2)}) async-start(), calls=%async_computation.25 | async-start | bytes 2457600 | tf_op jit(solution)/shard_map/all_gather | solution.py:252
  2727.6 59.7 %all-gather.26.cloned.1.call-start = ((), (), s32[]{:S(2)}) async-start(), calls=%async_computation.29 | async-start | bytes 2457600 | tf_op jit(solution)/shard_map/all_gather | solution.py:252
  2728.2 269.7 %all-reduce.17.cloned.1.call-start = ((), (), s32[]{:S(2)}) async-start(), calls=%async_computation.37 | async-start | bytes 2097152
  2841.2 158.3 %reduce-scatter.35.cloned.1.call-start = ((), (), s32[]{:S(2)}) async-start(), calls=%async_computation.31 | async-start | bytes 278528 | tf_op jit(solution)/shard_map/reduce_scatter | solution.py:309
  2845.1 176.4 %reduce-scatter.29.cloned.1.call-start = ((), (), s32[]{:S(2)}) async-start(), calls=%async_computation.26 | async-start | bytes 2457600 | tf_op jit(solution)/shard_map/reduce_scatter | solution.py:288
  2849.6 201.6 %reduce-scatter.33.cloned.1.call-start = ((), (), s32[]{:S(2)}) async-start(), calls=%async_computation.30 | async-start | bytes 2457600 | tf_op jit(solution)/shard_map/reduce_scatter | solution.py:288
  2880.3 505.8 %reduce-scatter.39.cloned.1.call-start = ((), (), s32[]{:S(2)}) async-start(), calls=%async_computation.33 | async-start | bytes 35651584 | tf_op jit(solution)/shard_map/reduce_scatter | solution.py:312
  2918.3 801.7 %reduce-scatter.41.cloned.1.call-start = ((), (), s32[]{:S(2)}) async-start(), calls=%async_computation.34 | async-start | bytes 35651584 | tf_op jit(solution)/shard_map/reduce_scatter | solution.py:315
  2988.8 868.6 %reduce-scatter.37.cloned.1.call-start = ((), (), s32[]{:S(2)}) async-start(), calls=%async_computation.32 | async-start | bytes 270336 | tf_op jit(solution)/shard_map/reduce_scatter | solution.py:324
  (116 other events, 1353.7 us)
Sparse Core Ops, SparseCore 0:
  56.1 27.7 all-gather.9
  86.0 27.9 all-gather.15
  146.3 24.3 reduce-scatter.18
  190.4 24.4 reduce-scatter.22
  220.7 27.9 all-gather.11
  250.1 27.9 all-gather.17
  279.6 307.6 all-gather.13
  589.5 28.0 all-gather.19
  619.1 27.9 all-gather.23
  2455.4 26.0 reduce-scatter.42
  2565.9 25.9 reduce-scatter.44
  2594.6 26.8 reduce-scatter.26
  2623.8 36.3 reduce-scatter.30
  2662.2 27.5 reduce-scatter.24
  2691.9 28.1 reduce-scatter.20
  2727.7 29.6 all-gather.21
  2759.4 27.9 all-gather.25
  2841.3 93.7 all-reduce.16
  2938.6 54.7 reduce-scatter.34
  2995.5 25.9 reduce-scatter.28
  3024.3 26.8 reduce-scatter.32
  3055.4 330.5 reduce-scatter.38
  3390.3 329.6 reduce-scatter.40
  3722.7 134.7 reduce-scatter.36
